TPU v7x, 128 devices: a whole 4x4x4 slice. The times are simulated.
128 devices in a mesh: date: 4 (over x), pix: 32 (over y, z, core).
Axes of the slice: x: 4, y: 4, z: 4, core: 2. Of those that a mesh axis runs over, the one named last changes fastest.
Arguments:
- stack: bfloat16 [64, 7, 256, 4096], P('date', None, None, 'pix'), may hold values from -8 to 8
- quality: int32 [64, 256, 4096], P('date', None, 'pix'), may hold values from 0 to 1073741823
- days: int32 [64], P('date'), may hold values from 8 to 1536, as said below
Outputs:
- coef: float32 [7, 8, 256, 4096], P(None, None, 'pix', 'date')
- score: float32 [7, 256, 4096], P(None, 'pix', 'date')
Inputs may be any that keep to these rules, and one draw needn't show every extreme that they name: `days`: strictly increasing.
All inputs are finite; a program needn't handle non-finite values.
Results may differ from a plain program's by a relative error of at most 0.0003.
Values may be sent and summed in bfloat16 or wider, within the bound.
A program may use at most 256 MiB of HBM per device.

v0:
```python
import jax
import jax.numpy as jnp
from jax import lax
from jax.sharding import Mesh
from jax.sharding import PartitionSpec as P

PIX = ("pix_0", "pix_1", "pix_2")
DATE_PIX = ("date", "pix_0", "pix_1", "pix_2")


RIDGE_TERM = 1.0
PAIR_LIST = [(first, second) for first in range(8) for second in range(first, 8)]


def by_axis(value, axes):
    for axis in axes:
        value = lax.psum(value, axis)
    return value


def pair_number(first, second):
    return PAIR_LIST.index((min(first, second), max(first, second)))


def design_matrix(days):
    moment_t = days.astype(jnp.float32)
    columns = [jnp.ones_like(moment_t), (moment_t - 512.0) / 512.0]
    for order in range(1, 4):
        phase = 2.0 * jnp.pi * order * moment_t / 365.25
        columns.append(jnp.cos(phase))
        columns.append(jnp.sin(phase))
    return jnp.stack(columns, 1)


def weights(quality):
    cloud = jnp.bitwise_and(jnp.right_shift(quality, 3), 1)
    level = jnp.bitwise_and(jnp.right_shift(quality, 8), 3)
    return (1 - cloud).astype(jnp.float32) / (1.0 + level.astype(jnp.float32))


def pair_products(design):
    return jnp.stack([design[:, first] * design[:, second] for first, second in PAIR_LIST], 1)


def chol_solve(gram, moment):
    lower = {}
    for first in range(8):
        for second in range(first + 1):
            total = gram[pair_number(first, second)]
            if first == second:
                total = total + RIDGE_TERM
            for inner in range(second):
                total = total - lower[first, inner] * lower[second, inner]
            if first == second:
                lower[first, first] = jnp.sqrt(total)
            else:
                lower[first, second] = total / lower[second, second]
    forward = []
    for first in range(8):
        total = moment[first]
        for inner in range(first):
            total = total - lower[first, inner][None, :] * forward[inner]
        forward.append(total / lower[first, first][None, :])
    backward = [None] * 8
    for first in range(7, -1, -1):
        total = forward[first]
        for inner in range(first + 1, 8):
            total = total - lower[inner, first][None, :] * backward[inner]
        backward[first] = total / lower[first, first][None, :]
    return jnp.stack(backward, 0)


def local(stack, quality, days):
    high = lax.Precision.HIGHEST
    bands = stack.shape[1]
    local_dates, all_rows, arrive_cols = (stack.shape[0], stack.shape[2], stack.shape[3])
    arrive_pixels = all_rows * arrive_cols
    design = design_matrix(days)
    weight = weights(quality).reshape(local_dates, arrive_pixels)
    samples = stack.reshape(local_dates, bands, arrive_pixels).astype(jnp.float32)
    gram_part = jnp.dot(pair_products(design).T, weight, precision=high)
    weighted = weight[:, None, :] * samples
    moment_part = jnp.dot(
        design.T, weighted.reshape(local_dates, bands * arrive_pixels), precision=high
    )
    square_part = jnp.sum(weighted * samples, 0)
    weight_part = jnp.sum(weight, 0)[None, :]
    stacked = jnp.concatenate(
        [gram_part, moment_part.reshape(8 * bands, arrive_pixels), square_part, weight_part], 0
    )
    stacked = stacked.reshape(stacked.shape[0], all_rows, arrive_cols)
    spread = lax.all_to_all(stacked, PIX, split_axis=1, concat_axis=2, tiled=True)
    summed = lax.psum_scatter(spread, "date", scatter_dimension=2, tiled=True)
    row_count, col_count = (summed.shape[1], summed.shape[2])
    pixels = row_count * col_count
    summed = summed.reshape(summed.shape[0], pixels)
    gram = summed[:36]
    moment = summed[36 : 36 + 8 * bands].reshape(8, bands, pixels)
    squares = summed[36 + 8 * bands : 36 + 9 * bands]
    wsum = summed[36 + 9 * bands]
    coef_flat = chol_solve(gram, moment)
    ssr = squares - 2.0 * jnp.sum(coef_flat * moment, 0)
    for first in range(8):
        for second in range(8):
            ssr = (
                ssr
                + gram[pair_number(first, second)][None, :] * coef_flat[first] * coef_flat[second]
            )
    total_ssr, total_weight = (by_axis(jnp.sum(ssr, 1), DATE_PIX), by_axis(jnp.sum(wsum), DATE_PIX))
    sigma2 = total_ssr / total_weight
    score = jnp.sqrt(ssr / (wsum[None, :] + 1.0)) / jnp.sqrt(sigma2)[:, None]
    coef = jnp.transpose(coef_flat.reshape(8, bands, row_count, col_count), (1, 0, 2, 3))
    return (coef, score.reshape(bands, row_count, col_count))


def solution(mesh):
    finer = Mesh(
        mesh.devices.reshape(mesh.shape["date"], 4, 4, 2), ("date", "pix_0", "pix_1", "pix_2")
    )
    return jax.shard_map(
        local,
        mesh=finer,
        in_specs=(P("date", None, None, PIX), P("date", None, PIX), P("date")),
        out_specs=(P(None, None, PIX, "date"), P(None, PIX, "date")),
        check_vma=False,
    )
```

profile of v0, /device:TPU:1, one launch (start us, length us, event | category | flops | bytes accessed | tf_op | source)
XLA Modules:
  0.0 501.0 jit_solution(10928785198846410375)
XLA Ops:
  7.2 2.3 fusion.176
  9.6 5.1 %fusion = f32[7,256,128]{2,1,0:T(8,128)S(1)} fusion(f32[16,256,128]{2,1,0:T(8,128)S(1)} %get-tuple-element.149, bf16[16,7,256,128]{3,2,1,0:T(8,128)(2,1)} %param.3), kind=kLoop, calls=%fused_computation.1 | loop fusion | flops 14450688 | bytes 10354688 | tf_op jit(solution)/shard_map/reduce_sum | solution.py:86
  16.5 2.5 copy.392
  19.0 9.1 %mul.6375 = f32[16,7,32768]{2,1,0:T(8,128)} broadcast(f32[16,32768]{1,0:T(8,128)} %bitcast.766), dimensions={0,2} | broadcast | bytes 16777216 | tf_op jit(solution)/shard_map/mul | solution.py:82
  28.1 19.7 %copy.189 = f32[2,8,7,32768]{3,1,2,0:T(8,128)} copy(f32[2,8,7,32768]{3,2,1,0:T(8,128)} %bitcast.761) | data formatting | bytes 29360128
  47.8 9.7 %convert.1 = f32[2,8,1792,128]{3,2,1,0:T(8,128)} convert(bf16[2,8,1792,128]{3,2,1,0:T(8,128)(2,1)} %bitcast.764) | non-fusion elementwise | flops 3670016 | bytes 22020096
  57.5 26.8 %fusion.1 = f32[8,229376]{1,0:T(8,128)} fusion(f32[16,8]{1,0:T(8,128)S(1)} %stack.167, f32[16,229376]{1,0:T(8,128)} %bitcast.760, f32[2,8,1792,128]{3,2,1,0:T(8,128)} %convert.1), kind=kOutput, calls=%fused_computation.3 | convolution fusion | flops 355991552 | bytes 36700672 | tf_op jit(solution)/shard_map/dot_general | solution.py:83
  84.3 7.2 %concatenate.9 = f32[56,256,128]{2,1,0:T(8,128)} reshape(f32[8,229376]{1,0:T(8,128)} %fusion.1) | data formatting | bytes 14680064 | tf_op jit(solution)/shard_map/concatenate | solution.py:88
  91.5 10.5 %copy.183 = f32[56,256,128]{2,0,1:T(8,128)} copy(f32[56,256,128]{2,1,0:T(8,128)} %concatenate.9) | data formatting | bytes 14680064 | tf_op jit(solution)/shard_map/concatenate | solution.py:88
  108.9 5.1 %fusion.3 = f32[36,256,128]{2,0,1:T(8,128)S(1)} fusion(f32[2,256,8,128]{3,2,1,0:T(8,128)S(1)} %bitcast.767, f32[16,36]{1,0:T(8,128)} %stack.166), kind=kOutput, calls=%fused_computation.8 | convolution fusion | flops 226492416 | bytes 6818048 | tf_op jit(solution)/shard_map/dot_general | solution.py:81
  114.0 2.1 pad_maximum_fusion
  116.1 161.4 %all_to_all.18 = f32[100,256,128]{2,0,1:T(8,128)} all-to-all(f32[100,256,128]{2,0,1:T(8,128)S(1)} %pad_maximum_fusion), channel_id=1, replica_groups=mesh['date'=4,'pix_0'=4,'pix_1'=4,'pix_2'=2] {'pix_0','pix_1','pix_2'}, dimensions={1} | all-to-all | bytes 26214400 | tf_op jit(solution)/shard_map/all_to_all | solution.py:92
  277.6 12.1 %copy.390 = f32[100,8,32,128]{3,1,2,0:T(8,128)} copy(f32[100,8,32,128]{3,0,1,2:T(8,128)} %bitcast.762) | data formatting | bytes 26214400 | tf_op jit(solution)/shard_map/all_to_all | solution.py:92
  289.6 116.3 %reduce-scatter.2.cloned.1.call-done = f32[100,8,1024]{2,1,0:T(8,128)} async-done(((f32[100,8,4096]{2,1,0:T(8,128)}), f32[100,8,1024]{2,1,0:T(8,128)}) %reduce-scatter.2.cloned.1.call-update) | async-done | bytes 3276816 | tf_op jit(solution)/shard_map/reduce_scatter | solution.py:93
  406.0 2.0 add_bitcast_fusion
  408.6 2.0 fusion.177
  413.4 1.8 squeeze.230
  442.6 3.2 reshape.15694
  446.0 2.6 multiply_reduce_fusion
  450.3 4.8 fusion.149
  457.5 7.2 %all-reduce.2 = (f32[7]{0:T(128)S(1)}, f32[]{:T(128)}) all-reduce(f32[7]{0:T(128)S(1)} %get-tuple-element.18, f32[]{:T(128)} %get-tuple-element.196), channel_id=1, replica_groups=mesh['date'=4,'pix_0'=4,'pix_1'=4,'pix_2'=2] {'date'}, use_global_device_ids=true, to_apply=%region_5.0 | all-reduce | flops 8 | bytes 64 | tf_op jit(solution)/shard_map/psum | solution.py:17
  464.6 9.1 %all-reduce.1 = (f32[7]{0:T(128)S(1)}, f32[]{:T(128)}) all-reduce(f32[7]{0:T(128)S(1)} %get-tuple-element.14, f32[]{:T(128)} %get-tuple-element.15), channel_id=1, replica_groups=mesh['date'=4,'pix_0'=4,'pix_1'=4,'pix_2'=2] {'pix_0'}, use_global_device_ids=true, to_apply=%region_6.0 | all-reduce | flops 8 | bytes 64 | tf_op jit(solution)/shard_map/psum | solution.py:17
  473.7 9.3 %all-reduce = (f32[7]{0:T(128)S(1)}, f32[]{:T(128)}) all-reduce(f32[7]{0:T(128)S(1)} %get-tuple-element.12, f32[]{:T(128)} %get-tuple-element.13), channel_id=1, replica_groups=mesh['date'=4,'pix_0'=4,'pix_1'=4,'pix_2'=2] {'pix_1'}, use_global_device_ids=true, to_apply=%region_7.0 | all-reduce | flops 8 | bytes 64 | tf_op jit(solution)/shard_map/psum | solution.py:17
  482.9 9.5 %all-reduce.3 = (f32[7]{0:T(128)S(1)}, f32[]{:T(128)}) all-reduce(f32[7]{0:T(128)S(1)} %get-tuple-element.10, f32[]{:T(128)} %get-tuple-element.11), channel_id=1, replica_groups=mesh['date'=4,'pix_0'=4,'pix_1'=4,'pix_2'=2] {'pix_2'}, use_global_device_ids=true, to_apply=%region_8.0 | all-reduce | flops 8 | bytes 64 | tf_op jit(solution)/shard_map/psum | solution.py:17
  (279 shorter events, 43.9 us)
Async XLA Ops:
  7.2 398.8 %reduce-scatter.2.cloned.1.call-start = ((), (), s32[]{:S(2)}) async-start(), calls=%async_computation.2 | async-start | bytes 16384000 | tf_op jit(solution)/shard_map/reduce_scatter | solution.py:93
  9.6 5.7 %copy-start.91 = (s32[16]{0:T(128)S(1)}, s32[16]{0:T(128)}, u32[]{:S(2)}) copy-start(s32[16]{0:T(128)} %param.5) | copy-start | bytes 196
  91.5 17.4 %copy-start.2 = (f32[2,8,256,128]{3,1,2,0:T(8,128)S(1)}, f32[2,8,256,128]{3,1,2,0:T(8,128)}, u32[]{:S(2)}) copy-start(f32[2,8,256,128]{3,1,2,0:T(8,128)} %copy.392) | copy-start | bytes 6291460
  108.9 5.1 %copy-start.1 = (f32[56,256,128]{2,0,1:T(8,128)S(1)}, f32[56,256,128]{2,0,1:T(8,128)}, u32[]{:S(2)}) copy-start(f32[56,256,128]{2,0,1:T(8,128)} %copy.183) | copy-start | bytes 22020100
  406.0 9.2 %copy-start = (f32[100,8,1024]{2,1,0:T(8,128)S(1)}, f32[100,8,1024]{2,1,0:T(8,128)}, u32[]{:S(2)}) copy-start(f32[100,8,1024]{2,1,0:T(8,128)} %reduce-scatter.2.cloned.1.call-done) | copy-start | bytes 9830404
  416.6 3.6 copy-start.21
  416.6 4.4 copy-start.9
  416.6 4.4 copy-start.19
  417.3 3.6 copy-start.39
  417.3 3.6 copy-start.41
  417.3 3.7 copy-start.43
  417.3 3.7 copy-start.45
  417.3 4.5 copy-start.17
  417.3 4.5 copy-start.37
  418.0 3.7 copy-start.11
  418.0 3.7 copy-start.52
  418.0 5.1 %copy-start.30 = (f32[8,1024]{1,0:T(8,128)}, f32[8,1024]{1,0:T(8,128)S(1)}, u32[]{:S(2)}) copy-start(f32[8,1024]{1,0:T(8,128)S(1)} %rsqrt_multiply_fusion.39) | copy-start | bytes 98308
  418.8 4.4 copy-start.15
  418.8 4.4 copy-start.65
  445.9 3.1 copy-start.40
  445.9 3.1 copy-start.42
  445.9 3.1 copy-start.44
  445.9 3.1 copy-start.46
  456.0 37.2 %copy-start.85 = (f32[8,1024]{1,0:T(8,128)S(1)}, f32[8,1024]{1,0:T(8,128)}, u32[]{:S(2)}) copy-start(f32[8,1024]{1,0:T(8,128)} %get-tuple-element.177) | copy-start | bytes 98308
  (69 other events, 136.5 us)
Sparse Core Ops, SparseCore 0:
  289.8 116.1 reduce-scatter.1
where the time goes:
time: 511 us; the launch traced here: 501 us
  blocking collectives  196 us (38%)
  waiting for transfers between devices  116 us (23%)
  local copies, waits for them, and re-layouts  93.4 us (18%)
  other arithmetic  47.2 us (9%)
  matrix products  31.9 us (6%)
  between operations  15.6 us (3%)
    all_to_all x1, blocking collectives, local(): lax.all_to_all(stacked, PIX, split_axis=1, concat_axis=2, tiled=True)  161 us
    reduce_scatter x1, waiting for transfers between devices, local(): summed = lax.psum_scatter(spread, 'date', scatter_dimension=2, tiled=True)  116 us
    psum x4, blocking collectives, by_axis(): value = lax.psum(value, axis)  35 us
    dot_general x1, matrix products, local(): jnp.dot(design.T, weighted.reshape(local_dates, bands * arrive_pixels), p...  26.8 us
    unnamed x194, local copies, waits for them, and re-layouts  26.4 us
    concatenate x2, local copies, waits for them, and re-layouts, local(): jnp.concatenate([gram_part, moment_part.reshape(8 * bands, arrive_pixels)...  17.6 us
    unnamed x10, other arithmetic  14.3 us
    squeeze x8, local copies, waits for them, and re-layouts, chol_solve(): total = moment[first]  13.4 us
  transfers between devices with their start and end apart: 1, of which 1 were waited for; matrix products, arithmetic and copies ran while one was open for 0% of the time, Pallas kernels for 0%

commit v1 on v0

v1 whole, which is shorter than its diff:
```python
import jax
import jax.numpy as jnp
from jax import lax
from jax.experimental import pallas as pl
from jax.experimental.pallas import tpu as pltpu
from jax.sharding import PartitionSpec as P

MESH = pl.DeviceIdType.MESH
F32 = jnp.float32
BF16 = jnp.bfloat16

BANDS = 7
GROUP = 16
PARTS = 4
DPART = GROUP // PARTS
CHUNKS = 4
STEPS = CHUNKS * PARTS
SCALE = 12.0
PAIRS = [(i, j) for i in range(8) for j in range(i, 8)]


def pair(i, j):
    return PAIRS.index((min(i, j), max(i, j)))


def design_matrix(days):
    moment_t = days.astype(F32)
    columns = [jnp.ones_like(moment_t), (moment_t - 512.0) / 512.0]
    for order in range(1, 4):
        phase = 2.0 * jnp.pi * order * moment_t / 365.25
        columns.append(jnp.cos(phase))
        columns.append(jnp.sin(phase))
    return jnp.stack(columns, 1)


def fit_kernel(
    stack, quality, design, coef_out, score_out,
    mid, midw, far, farw, wout, qv, dbuf, dfull, acc, gram, low, res, sres, sstage, arsum, arsrc, arbuf,
    q_sem, l_sem, d_loc, ys, yr, yws, ywr, xs, xr, xws, xwr, ds_, dr_, cs, cr, ss, sr, c_loc, as_, ar_,
):
    x = lax.axis_index("date")
    p = lax.axis_index("pix")
    y = lax.div(p, 8)
    z = lax.rem(lax.div(p, 2), 4)
    c = lax.rem(p, 2)

    def pix(py, pz, pc):
        return (py * 4 + pz) * 2 + pc

    y_peers = [(x, pix(lax.rem(y + t, 4), z, c)) for t in range(1, 4)]
    x_peers = [(lax.rem(x + t, 4), p) for t in range(1, 4)]
    z_peers = [
        (x, pix(y, lax.rem(z + e // 2, 4), lax.rem(c + e % 2, 2))) for e in range(1, 8)
    ]

    def remote(src, dst, send, recv, dev):
        return pltpu.make_async_remote_copy(
            src_ref=src, dst_ref=dst, send_sem=send, recv_sem=recv,
            device_id=dev, device_id_type=MESH,
        )

    q_copy = pltpu.make_async_copy(quality, qv, q_sem)
    q_copy.start()
    d_copy = pltpu.make_async_copy(design, dbuf.at[0], d_loc)
    d_copy.start()

    barrier = pltpu.get_barrier_semaphore()
    for dev in y_peers + x_peers + z_peers:
        pl.semaphore_signal(barrier, inc=1, device_id=dev, device_id_type=MESH)
    pl.semaphore_wait(barrier, 13)

    def chunk_row(ry, t):
        return pl.multiple_of(ry * 64 + lax.rem(z + 1 + t, 4) * 16, 16)

    def y_copy(s, t, q, tp):
        ry = lax.rem(y + tp, 4)
        return remote(
            stack.at[pl.ds(q * DPART, DPART), :, pl.ds(chunk_row(ry, t), 16), :],
            mid.at[4 - tp, t, pl.ds(q * DPART, DPART)],
            ys.at[s, tp - 1], yr.at[s, 3 - tp], y_peers[tp - 1],
        )

    def y_local(s, t, q):
        return pltpu.make_async_copy(
            stack.at[pl.ds(q * DPART, DPART), :, pl.ds(chunk_row(y, t), 16), :],
            mid.at[0, t, pl.ds(q * DPART, DPART)],
            l_sem.at[s],
        )

    def yw_copy(t, tp):
        return remote(
            wout.at[tp - 1, t], midw.at[4 - tp, t],
            yws.at[t, tp - 1], ywr.at[t, 3 - tp], y_peers[tp - 1],
        )

    def x_copy(s, t, q, tp):
        i = lax.rem(x + tp - y + 4, 4)
        return remote(
            mid.at[i, t, pl.ds(q * DPART, DPART)],
            far.at[3 - tp, t, pl.ds(q * DPART, DPART)],
            xs.at[s, tp - 1], xr.at[s, 3 - tp], x_peers[tp - 1],
        )

    def xw_copy(t, tp):
        i = lax.rem(x + tp - y + 4, 4)
        return remote(
            midw.at[i, t], farw.at[3 - tp, t],
            xws.at[t, tp - 1], xwr.at[t, 3 - tp], x_peers[tp - 1],
        )

    def d_remote(tp):
        return remote(design, dbuf.at[4 - tp], ds_.at[tp - 1], dr_.at[3 - tp], x_peers[tp - 1])

    def y_start(s):
        t = lax.div(s, PARTS)
        q = lax.rem(s, PARTS)
        for tp in (2, 1, 3):
            y_copy(s, t, q, tp).start()
        y_local(s, t, q).start()

    y_start(0)
    for tp in range(1, 4):
        d_remote(tp).start()

    q_copy.wait()

    def encode(n, carry):
        tp = lax.div(n, CHUNKS)
        t = lax.rem(n, CHUNKS)
        bits = qv[:, pl.ds(chunk_row(lax.rem(y + tp, 4), t), 16), :]
        level = jnp.bitwise_and(jnp.right_shift(bits, 8), 3)
        clear = jnp.bitwise_and(bits, 8) == 0
        code = jnp.where(level == 0, 12.0, jnp.where(level == 1, 6.0, jnp.where(level == 2, 4.0, 3.0)))
        code = jnp.where(clear, code, 0.0).astype(BF16)

        @pl.when(tp == 0)
        def _():
            midw[0, t] = code

        @pl.when(tp > 0)
        def _():
            wout[tp - 1, t] = code

        return carry

    lax.fori_loop(0, 4 * CHUNKS, encode, 0)

    def yw_start(t):
        for tp in (2, 1, 3):
            yw_copy(t, tp).start()

    yw_start(0)
    y_start(1)
    y_start(2)

    d_copy.wait()
    for tp in range(1, 4):
        d_remote(tp).wait_recv()

    def spread(n, carry):
        g = lax.div(n, GROUP)
        d = lax.rem(n, GROUP)
        for i in range(8):
            dfull[g, d, i] = jnp.broadcast_to(dbuf[g, d, pl.ds(i, 1), :], (8, 128))
        return carry

    lax.fori_loop(0, 4 * GROUP, spread, 0)
    arsum[...] = jnp.zeros_like(arsum)

    home = lax.rem(x - y + 4, 4)

    def column(g, d, i):
        v = dfull[g, d, i]
        return jnp.concatenate([v, v], 0)

    def groups(t):
        out = [(mid.at[home, t], midw.at[home, t])]
        for j in range(1, 4):
            out.append((far.at[j - 1, t], farw.at[j - 1, t]))
        return out

    def factor(t):
        refs = groups(t)
        for rows in ((0, 1), (2, 3), (4, 5, 6, 7)):
            wanted = [(i, j) for i in rows for j in range(i, 8)]

            def add(d, sums, rows=rows, wanted=wanted):
                sums = list(sums)
                for g in range(4):
                    w = refs[g][1][d].astype(F32)
                    cols = {k: column(g, d, k) for k in range(rows[0], 8)}
                    for i in rows:
                        wd = w if i == 0 else w * cols[i]
                        for j in range(i, 8):
                            n = wanted.index((i, j))
                            sums[n] = sums[n] + (wd if j == 0 else wd * cols[j])
                return tuple(sums)

            sums = lax.fori_loop(
                0, GROUP, add, tuple(jnp.zeros((16, 128), F32) for _ in wanted)
            )
            for n, (i, j) in enumerate(wanted):
                gram[pair(i, j)] = sums[n]
        for half in (0, 8):
            lower = {}
            for j in range(8):
                total = gram[pair(j, j), half:half + 8, :] + SCALE
                for k in range(j):
                    total = total - lower[j, k] * lower[j, k]
                inverse = 1.0 / jnp.sqrt(total)
                low[pair(j, j), half:half + 8, :] = inverse
                for i in range(j + 1, 8):
                    total = gram[pair(j, i), half:half + 8, :]
                    for k in range(j):
                        total = total - lower[i, k] * lower[j, k]
                    lower[i, j] = total * inverse
                    low[pair(j, i), half:half + 8, :] = lower[i, j]
        arsum[7] = arsum[7] + gram[0, 0:8, :] + gram[0, 8:16, :]

    def moments(t, q):
        refs = groups(t)

        def band(b, carry):
            sums = [acc[b, n] for n in range(9)]
            for g in range(4):
                for dd in range(DPART):
                    d = q * DPART + dd
                    v = refs[g][0][d, b].astype(F32)
                    wv = refs[g][1][d].astype(F32) * v
                    sums[8] = sums[8] + wv * v
                    sums[0] = sums[0] + wv
                    for i in range(1, 8):
                        sums[i] = sums[i] + wv * column(g, d, i)
            for n in range(9):
                acc[b, n] = sums[n]
            return carry

        lax.fori_loop(0, BANDS, band, 0)

    def solve(t):
        def band(b, carry):
            fit = []
            explained = None
            for i in range(8):
                total = acc[b, i]
                for k in range(i):
                    total = total - low[pair(k, i)] * fit[k]
                total = total * low[pair(i, i)]
                fit.append(total)
                explained = total * total if i == 0 else explained + total * total
            for i in range(7, -1, -1):
                total = fit[i]
                for k in range(i + 1, 8):
                    total = total - low[pair(i, k)] * fit[k]
                total = total * low[pair(i, i)]
                fit[i] = total
                res[t, 0, b, i] = total[0:8, :]
                res[t, 1, b, i] = total[8:16, :]
                explained = explained + SCALE * total * total
            ssr = jnp.maximum(acc[b, 8] - explained, 0.0)
            arsum[b] = arsum[b] + ssr[0:8, :] + ssr[8:16, :]
            ratio = jnp.sqrt(ssr / (gram[0] + SCALE))
            sres[t, 0, b] = ratio[0:8, :]
            sres[t, 1, b] = ratio[8:16, :]
            return carry

        lax.fori_loop(0, BANDS, band, 0)

    def lanes(pz, pc):
        return pl.ds(pl.multiple_of((pz * 2 + pc) * 128, 128), 128)

    def out_copies(t, half, slot, dev):
        return (
            remote(sres.at[t, half], sstage.at[z * 2 + c], ss.at[t, half], sr.at[t, slot], dev),
            remote(res.at[t, half], coef_out.at[:, :, :, lanes(z, c)], cs.at[t, half], cr.at[t, slot], dev),
        )

    def step(s, carry):
        @pl.when(s < STEPS)
        def _():
            t = lax.div(s, PARTS)
            q = lax.rem(s, PARTS)

            @pl.when(q == 0)
            def _():
                for tp in range(1, 4):
                    yw_copy(t, tp).wait_recv()
                for tp in (2, 1, 3):
                    xw_copy(t, tp).start()

            y_local(s, t, q).wait()
            for tp in range(1, 4):
                y_copy(s, t, q, tp).wait_recv()
            for tp in (2, 1, 3):
                x_copy(s, t, q, tp).start()

            @pl.when(s + 3 < STEPS)
            def _():
                @pl.when(lax.rem(s + 3, PARTS) == 0)
                def _():
                    yw_start(lax.div(s + 3, PARTS))

                y_start(s + 3)

        @pl.when(s > 0)
        def _():
            n = s - 1
            t = lax.div(n, PARTS)
            q = lax.rem(n, PARTS)

            @pl.when(q == 0)
            def _():
                for tp in range(1, 4):
                    xw_copy(t, tp).wait_recv()
                acc[...] = jnp.zeros_like(acc)
                factor(t)

            for tp in range(1, 4):
                x_copy(n, t, q, tp).wait_recv()
            moments(t, q)

            @pl.when(q == PARTS - 1)
            def _():
                solve(t)

                @pl.when(t < CHUNKS - 1)
                def _():
                    for half in range(2):
                        dev = (x, pix(y, lax.rem(z + 1 + t, 4), half))
                        for copy in out_copies(t, half, c, dev):
                            copy.start()

        return carry

    lax.fori_loop(0, STEPS + 1, step, 0)

    last = CHUNKS - 1
    twin = (x, pix(y, z, 1 - c))
    arsrc[0] = jnp.sum(arsum[...], axis=1)

    def gather(stage, peers, first):
        copies = [
            remote(arsrc.at[stage], arbuf.at[first + n], as_.at[first + n], ar_.at[first + n], dev)
            for n, dev in enumerate(peers)
        ]
        for copy in copies:
            copy.start()
        return copies

    copies = gather(0, z_peers, 0)
    twin_copies = out_copies(last, 1 - c, 0, twin)
    for copy in twin_copies:
        copy.start()
    own = pltpu.make_async_copy(res.at[last, c], coef_out.at[:, :, :, lanes(z, c)], c_loc)
    own.start()
    sstage[z * 2 + c] = sres[last, c]
    started = list(copies)
    for stage, peers, first in ((1, y_peers, 7), (2, x_peers, 10)):
        for copy in copies:
            copy.wait_recv()
        total = arsrc[stage - 1]
        for n in range(len(copies)):
            total = total + arbuf[first - len(copies) + n]
        arsrc[stage] = total
        copies = gather(stage, peers, first)
        started += copies
    for copy in copies:
        copy.wait_recv()
    total = arsrc[2]
    for n in range(3):
        total = total + arbuf[10 + n]
    total = jnp.sum(total, axis=1, keepdims=True)
    inverse = 1.0 / jnp.sqrt(total / total[7:8, :])

    for t in range(CHUNKS - 1):
        for half in range(2):
            dev = (x, pix(y, lax.rem(z + 1 + t, 4), half))
            for copy in out_copies(t, half, half, dev):
                copy.wait()
    for copy in twin_copies:
        copy.wait()
    own.wait()
    for b in range(BANDS):
        factor_b = jnp.broadcast_to(inverse[b:b + 1, :], (8, 128))
        for n in range(8):
            score_out[b, :, n * 128:(n + 1) * 128] = sstage[n, b] * factor_b

    for copy in started:
        copy.wait_send()
    for tp in range(1, 4):
        d_remote(tp).wait_send()

    def drain(s, carry):
        t = lax.div(s, PARTS)
        q = lax.rem(s, PARTS)
        for tp in range(1, 4):
            y_copy(s, t, q, tp).wait_send()
            x_copy(s, t, q, tp).wait_send()

        @pl.when(q == 0)
        def _():
            for tp in range(1, 4):
                yw_copy(t, tp).wait_send()
                xw_copy(t, tp).wait_send()

        return carry

    lax.fori_loop(0, STEPS, drain, 0)


def local(stack, quality, days):
    design = jnp.broadcast_to(design_matrix(days)[:, :, None], (GROUP, 8, 128))
    dma = pltpu.SemaphoreType.DMA
    vmem = pltpu.VMEM
    hbm = pl.BlockSpec(memory_space=pltpu.HBM)
    return pl.pallas_call(
        fit_kernel,
        out_shape=(
            jax.ShapeDtypeStruct((BANDS, 8, 8, 1024), F32),
            jax.ShapeDtypeStruct((BANDS, 8, 1024), F32),
        ),
        in_specs=[hbm, hbm, hbm],
        out_specs=(hbm, pl.BlockSpec(memory_space=pltpu.VMEM)),
        scratch_shapes=[
            vmem((4, CHUNKS, GROUP, BANDS, 16, 128), BF16),
            vmem((4, CHUNKS, GROUP, 16, 128), BF16),
            vmem((3, CHUNKS, GROUP, BANDS, 16, 128), BF16),
            vmem((3, CHUNKS, GROUP, 16, 128), BF16),
            vmem((3, CHUNKS, GROUP, 16, 128), BF16),
            vmem((GROUP, 256, 128), jnp.int32),
            vmem((4, GROUP, 8, 128), F32),
            vmem((4, GROUP, 8, 8, 128), F32),
            vmem((BANDS, 9, 16, 128), F32),
            vmem((36, 16, 128), F32),
            vmem((36, 16, 128), F32),
            vmem((CHUNKS, 2, BANDS, 8, 8, 128), F32),
            vmem((CHUNKS, 2, BANDS, 8, 128), F32),
            vmem((8, BANDS, 8, 128), F32),
            vmem((8, 8, 128), F32),
            vmem((3, 8, 128), F32),
            vmem((13, 8, 128), F32),
            dma, dma((STEPS,)), dma,
            dma((STEPS, 3)), dma((STEPS, 3)), dma((CHUNKS, 3)), dma((CHUNKS, 3)),
            dma((STEPS, 3)), dma((STEPS, 3)), dma((CHUNKS, 3)), dma((CHUNKS, 3)),
            dma((3,)), dma((3,)),
            dma((CHUNKS, 2)), dma((CHUNKS, 2)), dma((CHUNKS, 2)), dma((CHUNKS, 2)),
            dma, dma((13,)), dma((13,)),
        ],
        compiler_params=pltpu.CompilerParams(
            collective_id=0, has_side_effects=True, vmem_limit_bytes=48 * 1024 * 1024
        ),
        name="fit",
    )(stack, quality, design)


def solution(mesh):
    return jax.shard_map(
        local,
        mesh=mesh,
        in_specs=(P("date", None, None, "pix"), P("date", None, "pix"), P("date")),
        out_specs=(P(None, None, "pix", "date"), P(None, "pix", "date")),
        check_vma=False,
    )
```

time: 511 us -> 130 us (0.25); the launches traced: 501 us -> 129 us
  blocking collectives: 196 us -> 0 us
  Pallas kernels: 0 us -> 124 us
  waiting for transfers between devices: 116 us -> 0 us
  local copies, waits for them, and re-layouts: 93.4 us -> 3.7 us
  other arithmetic: 47.2 us -> 0.71 us
  matrix products: 31.9 us -> 0 us
  between operations: 15.6 us -> 0.66 us
    all_to_all x1 -> x0, blocking collectives: 161 us -> none  [local(): lax.all_to_all(stacked, PIX, split_axis=1, concat_axis=2, tiled=True)]
    pallas_call x0 -> x1, Pallas kernels: none -> 124 us  [local(): pl.pallas_call(fit_kernel, out_shape=(jax.ShapeDtypeStruct((BANDS, 8, 8,...]
    reduce_scatter x1 -> x0, waiting for transfers between devices: 116 us -> none  [local(): summed = lax.psum_scatter(spread, 'date', scatter_dimension=2, tiled=True)]
    psum x4 -> x0, blocking collectives: 35 us -> none  [by_axis(): value = lax.psum(value, axis)]
    dot_general x2 -> x0, matrix products: 31.9 us -> none  [the longest x1 26.8 us: local(): jnp.dot(design.T, weighted.reshape(local_dates, bands * arrive_pixels), p...]
    unnamed x194 -> x4, local copies, waits for them, and re-layouts: 26.4 us -> 3.51 us
    concatenate x2 -> x0, local copies, waits for them, and re-layouts: 17.6 us -> none  [local(): jnp.concatenate([gram_part, moment_part.reshape(8 * bands, arrive_pixels)...]
    reduce_sum x5 -> x0, other arithmetic: 15.6 us -> none  [the longest x1 5.12 us: local(): square_part = jnp.sum(weighted * samples, 0)]
  transfers between devices with their start and end apart: 1 -> 0, of which waited for: 1 -> 0; matrix products, arithmetic and copies ran while one was open for 0% -> 0% of each run, Pallas kernels for 0% -> 0%
where the time goes in v1:
time: 130 us; the launch traced here: 129 us
  Pallas kernels  124 us (95%)
  local copies, waits for them, and re-layouts  3.7 us (3%)
    pallas_call x1, Pallas kernels, local(): pl.pallas_call(fit_kernel, out_shape=(jax.ShapeDtypeStruct((BANDS, 8, 8,...  124 us
    unnamed x4, local copies, waits for them, and re-layouts  3.51 us

profile of v1, /device:TPU:1, one launch (start us, length us, event | category | flops | bytes accessed | tf_op | source)
XLA Modules:
  0.0 129.4 jit_solution(385718234526425935)
XLA Ops:
  0.6 0.7 sine_bitcast_fusion
  1.4 0.1 copy.5
  1.5 0.1 broadcast_in_dim.2.design
  1.5 0.0 copy-start
  1.5 1.6 %copy-done = s32[16,256,128]{2,1,0:T(8,128)S(1)} copy-done((s32[16,256,128]{2,1,0:T(8,128)S(1)}, s32[16,256,128]{2,1,0:T(8,128)}, u32[]{:S(2)}) %copy-start) | copy-done | bytes 2097176
  3.1 124.3 %fit.1 = (f32[7,8,8,1024]{3,2,1,0:T(8,128)S(1)}, f32[7,8,1024]{2,1,0:T(8,128)S(1)}) custom-call(bf16[16,7,256,128]{3,2,1,0:T(8,128)(2,1)} %stack.33, s32[16,256,128]{2,1,0:T(8,128)S(1)} %copy-done, f32[16,8,128]{2,1,0:T(8,128)S(1)} %broadcast_in_dim.2.design), custom_call_target="tpu_custom_call" | custom-call | tf_op jit(solution)/shard_map/fit/pallas_call | solution.py:416
  127.5 1.2 copy.8
  128.7 0.7 copy.9
  (2 shorter events, 0.0 us)
Async XLA Ops:
  1.5 1.6 %copy-start = (s32[16,256,128]{2,1,0:T(8,128)S(1)}, s32[16,256,128]{2,1,0:T(8,128)}, u32[]{:S(2)}) copy-start(s32[16,256,128]{2,1,0:T(8,128)} %quality.1) | copy-start | bytes 6291460

commit v2 on v1

v2 whole, which is shorter than its diff:
```python
import jax
import jax.numpy as jnp
from jax import lax
from jax.experimental import pallas as pl
from jax.experimental.pallas import tpu as pltpu
from jax.sharding import PartitionSpec as P

MESH = pl.DeviceIdType.MESH
F32 = jnp.float32
BF16 = jnp.bfloat16

BANDS = 7
GROUP = 16
PARTS = 4
DPART = GROUP // PARTS
CHUNKS = 4
STEPS = CHUNKS * PARTS
AHEAD = 3
LAG = 3
SCALE = 12.0
PAIRS = [(i, j) for i in range(8) for j in range(i, 8)]


def pair(i, j):
    return PAIRS.index((min(i, j), max(i, j)))


def design_matrix(days):
    moment_t = days.astype(F32)
    columns = [jnp.ones_like(moment_t), (moment_t - 512.0) / 512.0]
    for order in range(1, 4):
        phase = 2.0 * jnp.pi * order * moment_t / 365.25
        columns.append(jnp.cos(phase))
        columns.append(jnp.sin(phase))
    return jnp.stack(columns, 1)


def fit_kernel(
    stack, quality, design, coef_out, score_out,
    mid, midw, far, farw, carry, carryw, wout, qv, dbuf, dfull, own_sums, pass_sums, got_sums,
    gram, low, res, sres, yres, ysres, sstage, arsum, arsrc, arbuf,
    q_sem, l_sem, d_loc, ys, yr, yws, ywr, a_s, a_r, b_s, b_r, xs, xr, wa_s, wa_r, ws, wr, sm_s, sm_r,
    ds_, dr_, e_s, e_r, fc, fs, cs, cr, ss, sr, c_loc, as_, ar_,
):
    x = lax.axis_index("date")
    p = lax.axis_index("pix")
    y = lax.div(p, 8)
    z = lax.rem(lax.div(p, 2), 4)
    c = lax.rem(p, 2)
    last = CHUNKS - 1

    def pix(py, pz, pc):
        return (py * 4 + pz) * 2 + pc

    def right(n):
        return (lax.rem(x + n, 4), p)

    fore = 1 + 2 * c
    back = 3 - 2 * c
    fore_dev = right(fore)
    back_dev = right(back)
    home = lax.rem(x - y + 4, 4)
    fore_slot = lax.rem(x + fore - y + 4, 4)
    back_slot = lax.rem(x + back - y + 4, 4)
    far_slot = lax.rem(x + 2 - y + 4, 4)
    turn = lax.rem(x + 2 * c, 4)

    y_peers = [(x, pix(lax.rem(y + t, 4), z, c)) for t in range(1, 4)]
    x_peers = [right(t) for t in range(1, 4)]
    plane_peers = [
        (lax.rem(x + n // 4, 4), pix(lax.rem(y + n % 4, 4), z, c)) for n in range(1, 16)
    ]
    z_peers = [
        (x, pix(y, lax.rem(z + e // 2, 4), lax.rem(c + e % 2, 2))) for e in range(1, 8)
    ]

    def remote(src, dst, send, recv, dev):
        return pltpu.make_async_remote_copy(
            src_ref=src, dst_ref=dst, send_sem=send, recv_sem=recv,
            device_id=dev, device_id_type=MESH,
        )

    def dates(q):
        return pl.ds(q * DPART, DPART)

    def chunk_row(ry, t):
        return pl.multiple_of(ry * 64 + lax.rem(z + 1 + t, 4) * 16, 16)

    def first_local(q, i):
        ry = lax.rem(y + i + 2 * c, 4)
        return pltpu.make_async_copy(
            stack.at[dates(q), :, pl.ds(chunk_row(ry, 0), 16), :],
            mid.at[i, 0, dates(q)],
            l_sem.at[q, i],
        )

    def y_local(s, t, q):
        return pltpu.make_async_copy(
            stack.at[dates(q), :, pl.ds(chunk_row(y, t), 16), :],
            mid.at[0, t, dates(q)],
            l_sem.at[s, 0],
        )

    def y_copy(s, t, q, tp):
        ry = lax.rem(y + tp, 4)
        return remote(
            stack.at[dates(q), :, pl.ds(chunk_row(ry, t), 16), :],
            mid.at[4 - tp, t, dates(q)],
            ys.at[s, tp - 1], yr.at[s, 3 - tp], y_peers[tp - 1],
        )

    def yw_copy(t, tp):
        return remote(
            wout.at[tp - 1, t], midw.at[4 - tp, t],
            yws.at[t, tp - 1], ywr.at[t, 3 - tp], y_peers[tp - 1],
        )

    def a_copy(s, t, q):
        return remote(mid.at[far_slot, t, dates(q)], carry.at[t, dates(q)], a_s.at[s], a_r.at[s], fore_dev)

    def b_copy(s, t, q):
        return remote(mid.at[back_slot, t, dates(q)], far.at[2 * c, t, dates(q)], b_s.at[s], b_r.at[s], back_dev)

    def x_copy(q, tp):
        i = lax.rem(x + tp - y + 4, 4)
        return remote(
            mid.at[i, last, dates(q)], far.at[3 - tp, last, dates(q)],
            xs.at[q, tp - 1], xr.at[q, 3 - tp], x_peers[tp - 1],
        )

    def xw_copy(tp):
        i = lax.rem(x + tp - y + 4, 4)
        return remote(
            midw.at[i, last], farw.at[3 - tp, last],
            ws.at[last, tp - 1], wr.at[last, 3 - tp], x_peers[tp - 1],
        )

    def wa_copy(t):
        return remote(midw.at[far_slot, t], carryw.at[t], wa_s.at[t], wa_r.at[t], fore_dev)

    def wb_copy(t):
        return remote(midw.at[back_slot, t], farw.at[2 * c, t], ws.at[t, 0], wr.at[t, 2 * c], back_dev)

    def wc_copy(t):
        return remote(midw.at[fore_slot, t], farw.at[2 - 2 * c, t], ws.at[t, 1], wr.at[t, 2 - 2 * c], fore_dev)

    def wd_copy(t):
        return remote(carryw.at[t], farw.at[1, t], ws.at[t, 2], wr.at[t, 1], fore_dev)

    def sum_copy(t):
        return remote(pass_sums.at[t], got_sums.at[t], sm_s.at[t], sm_r.at[t], fore_dev)

    def d_remote(tp):
        return remote(design, dbuf.at[4 - tp], ds_.at[tp - 1], dr_.at[3 - tp], x_peers[tp - 1])

    def y_start(s):
        t = lax.div(s, PARTS)
        q = lax.rem(s, PARTS)
        for tp in (2, 1, 3):
            y_copy(s, t, q, tp).start()
        y_local(s, t, q).start()

    def yw_start(t):
        for tp in (2, 1, 3):
            yw_copy(t, tp).start()

    for i in range(4):
        first_local(0, i).start()
    q_copy = pltpu.make_async_copy(quality, qv, q_sem)
    q_copy.start()
    for q in range(1, PARTS):
        for i in range(4):
            first_local(q, i).start()
    d_copy = pltpu.make_async_copy(design, dbuf.at[0], d_loc)
    d_copy.start()

    barrier = pltpu.get_barrier_semaphore()
    for dev in y_peers + x_peers + z_peers:
        pl.semaphore_signal(barrier, inc=1, device_id=dev, device_id_type=MESH)
    pl.semaphore_wait(barrier, 13)

    y_start(PARTS)
    for i in range(4):
        first_local(0, i).wait()
    a_copy(0, 0, 0).start()
    b_copy(0, 0, 0).start()
    for tp in range(1, 4):
        d_remote(tp).start()

    q_copy.wait()

    def encode(n, carried):
        t = lax.div(n, 4)
        tp = lax.rem(n, 4)
        ry = lax.rem(y + tp + jnp.where(t == 0, 2 * c, 0), 4)
        bits = qv[:, pl.ds(chunk_row(ry, t), 16), :]
        level = jnp.bitwise_and(jnp.right_shift(bits, 8), 3)
        clear = jnp.bitwise_and(bits, 8) == 0
        code = jnp.where(level == 0, 12.0, jnp.where(level == 1, 6.0, jnp.where(level == 2, 4.0, 3.0)))
        code = jnp.where(clear, code, 0.0).astype(BF16)
        kept = jnp.logical_or(t == 0, tp == 0)

        @pl.when(kept)
        def _():
            midw[tp, t] = code

        @pl.when(jnp.logical_not(kept))
        def _():
            wout[tp - 1, t] = code

        return carried

    lax.fori_loop(0, 4 * CHUNKS, encode, 0)
    yw_start(1)
    for s in range(1, AHEAD):
        y_start(PARTS + s)
    arsum[...] = jnp.zeros_like(arsum)

    def column(g, d, i):
        v = dfull[g, d, i]
        return jnp.concatenate([v, v], 0)

    def columns():
        d_copy.wait()
        for tp in range(1, 4):
            d_remote(tp).wait_recv()

        def spread(n, carried):
            g = lax.div(n, GROUP)
            d = lax.rem(n, GROUP)
            row = dbuf[g, pl.ds(d, 1), :]
            for i in range(8):
                dfull[g, d, i] = jnp.broadcast_to(row[:, i:i + 1], (8, 128))
            return carried

        lax.fori_loop(0, 4 * GROUP, spread, 0)

    def factor(t):
        codes = [midw.at[home, t]] + [farw.at[j, t] for j in range(3)]
        for rows in ((0, 1), (2, 3), (4, 5, 6, 7)):
            wanted = [(i, j) for i in rows for j in range(i, 8)]

            def add(d, sums, rows=rows, wanted=wanted):
                sums = list(sums)
                for g in range(4):
                    w = codes[g][d].astype(F32)
                    cols = {k: column(g, d, k) for k in range(rows[0], 8)}
                    for i in rows:
                        wd = w if i == 0 else w * cols[i]
                        for j in range(i, 8):
                            n = wanted.index((i, j))
                            sums[n] = sums[n] + (wd if j == 0 else wd * cols[j])
                return tuple(sums)

            sums = lax.fori_loop(
                0, GROUP, add, tuple(jnp.zeros((16, 128), F32) for _ in wanted)
            )
            for n, (i, j) in enumerate(wanted):
                gram[t, pair(i, j)] = sums[n]
        for half in (0, 8):
            lower = {}
            for j in range(8):
                total = gram[t, pair(j, j), half:half + 8, :] + SCALE
                for k in range(j):
                    total = total - lower[j, k] * lower[j, k]
                inverse = 1.0 / jnp.sqrt(total)
                low[t, pair(j, j), half:half + 8, :] = inverse
                for i in range(j + 1, 8):
                    total = gram[t, pair(j, i), half:half + 8, :]
                    for k in range(j):
                        total = total - lower[i, k] * lower[j, k]
                    lower[i, j] = total * inverse
                    low[t, pair(j, i), half:half + 8, :] = lower[i, j]
        arsum[7] = arsum[7] + gram[t, 0, 0:8, :] + gram[t, 0, 8:16, :]

    def moments(acc, refs, q):
        def band(b, carried):
            sums = [acc[b, n] for n in range(9)]
            for values, codes, g in refs:
                for dd in range(DPART):
                    d = q * DPART + dd
                    v = values[d, b].astype(F32)
                    wv = codes[d].astype(F32) * v
                    sums[8] = sums[8] + wv * v
                    sums[0] = sums[0] + wv
                    for i in range(1, 8):
                        sums[i] = sums[i] + wv * column(g, d, i)
            for n in range(9):
                acc[b, n] = sums[n]
            return carried

        lax.fori_loop(0, BANDS, band, 0)

    def solve(t, passed):
        def band(b, carried):
            def total_of(n):
                total = own_sums[t, b, n]
                return total + got_sums[t, b, n] if passed else total

            fit = []
            explained = None
            for i in range(8):
                total = total_of(i)
                for k in range(i):
                    total = total - low[t, pair(k, i)] * fit[k]
                total = total * low[t, pair(i, i)]
                fit.append(total)
                explained = total * total if i == 0 else explained + total * total
            for i in range(7, -1, -1):
                total = fit[i]
                for k in range(i + 1, 8):
                    total = total - low[t, pair(i, k)] * fit[k]
                total = total * low[t, pair(i, i)]
                fit[i] = total
                res[t, 0, b, i] = total[0:8, :]
                res[t, 1, b, i] = total[8:16, :]
                explained = explained + SCALE * total * total
            ssr = jnp.maximum(total_of(8) - explained, 0.0)
            arsum[b] = arsum[b] + ssr[0:8, :] + ssr[8:16, :]
            ratio = jnp.sqrt(ssr / (gram[t, 0] + SCALE))
            sres[t, 0, b] = ratio[0:8, :]
            sres[t, 1, b] = ratio[8:16, :]
            return carried

        lax.fori_loop(0, BANDS, band, 0)

    def lanes(pz, pc):
        return pl.ds(pl.multiple_of((pz * 2 + pc) * 128, 128), 128)

    def out_copies(t, half, slot, dev):
        return (
            remote(sres.at[t, half], sstage.at[z * 2 + c], ss.at[t, half], sr.at[t, slot], dev),
            remote(res.at[t, half], coef_out.at[:, :, :, lanes(z, c)], cs.at[t, half], cr.at[t, slot], dev),
        )

    def y_results():
        slot = lax.rem(y - turn + 3, 4)
        dev = (x, pix(turn, z, c))
        return (
            remote(sres.at[0], ysres.at[slot], e_s.at[0], e_r.at[slot, 0], dev),
            remote(res.at[0], yres.at[slot], e_s.at[1], e_r.at[slot, 1], dev),
        )

    def y_arrival(slot):
        dev = (x, pix(turn, z, c))
        return (
            remote(sres.at[0], ysres.at[slot], e_s.at[0], e_r.at[slot, 0], dev),
            remote(res.at[0], yres.at[slot], e_s.at[1], e_r.at[slot, 1], dev),
        )

    def turned(i, half):
        dev = (lax.rem(y + i, 4), pix(y, lax.rem(z + 1, 4), half))
        src_score = sres.at[0, half] if i == 0 else ysres.at[i - 1, half]
        src = res.at[0, half] if i == 0 else yres.at[i - 1, half]
        return (
            remote(src_score, sstage.at[z * 2 + c], fs.at[i, half], sr.at[0, c], dev),
            remote(src, coef_out.at[:, :, :, lanes(z, c)], fc.at[i, half], cr.at[0, c], dev),
        )

    def step(s, carried):
        @pl.when(s < STEPS)
        def _():
            t = lax.div(s, PARTS)
            q = lax.rem(s, PARTS)

            @pl.when(jnp.logical_and(t == 0, q > 0))
            def _():
                for i in range(4):
                    first_local(q, i).wait()

            @pl.when(t > 0)
            def _():
                y_local(s, t, q).wait()
                for tp in range(1, 4):
                    y_copy(s, t, q, tp).wait_recv()

            @pl.when(jnp.logical_and(s > 0, t < last))
            def _():
                a_copy(s, t, q).start()
                b_copy(s, t, q).start()

            @pl.when(t == last)
            def _():
                for tp in (2, 1, 3):
                    x_copy(q, tp).start()

            @pl.when(q == 0)
            def _():
                @pl.when(t > 0)
                def _():
                    for tp in range(1, 4):
                        yw_copy(t, tp).wait_recv()

                @pl.when(t < last)
                def _():
                    wa_copy(t).start()
                    wb_copy(t).start()
                    wc_copy(t).start()

                @pl.when(t == last)
                def _():
                    for tp in (2, 1, 3):
                        xw_copy(tp).start()

            nxt = s + PARTS + AHEAD

            @pl.when(nxt < STEPS)
            def _():
                @pl.when(lax.rem(nxt, PARTS) == 0)
                def _():
                    yw_start(lax.div(nxt, PARTS))

                y_start(nxt)

        @pl.when(s >= LAG)
        def _():
            n = s - LAG
            t = lax.div(n, PARTS)
            q = lax.rem(n, PARTS)

            @pl.when(n == 0)
            def _():
                columns()

            @pl.when(q == 0)
            def _():
                own_sums[t] = jnp.zeros((BANDS, 9, 16, 128), F32)

                @pl.when(t < last)
                def _():
                    pass_sums[t] = jnp.zeros((BANDS, 9, 16, 128), F32)
                    wa_copy(t).wait_recv()
                    wd_copy(t).start()
                    wb_copy(t).wait_recv()

                @pl.when(t == last)
                def _():
                    for tp in range(1, 4):
                        xw_copy(tp).wait_recv()

            @pl.when(t < last)
            def _():
                a_copy(n, t, q).wait_recv()
                moments(
                    pass_sums.at[t],
                    [(mid.at[fore_slot, t], midw.at[fore_slot, t], 0), (carry.at[t], carryw.at[t], back)],
                    q,
                )

                @pl.when(q == PARTS - 1)
                def _():
                    sum_copy(t).start()

                b_copy(n, t, q).wait_recv()

            @pl.when(t == last)
            def _():
                for tp in range(1, 4):
                    x_copy(q, tp).wait_recv()
                moments(
                    own_sums.at[t],
                    [(far.at[1, t], farw.at[1, t], 2), (far.at[2 - 2 * c, t], farw.at[2 - 2 * c, t], back)],
                    q,
                )

            moments(
                own_sums.at[t],
                [(mid.at[home, t], midw.at[home, t], 0), (far.at[2 * c, t], farw.at[2 * c, t], fore)],
                q,
            )

            @pl.when(q == PARTS - 2)
            def _():
                @pl.when(t < last)
                def _():
                    wc_copy(t).wait_recv()
                    wd_copy(t).wait_recv()

                factor(t)

                @pl.when(t > 0)
                def _():
                    sum_copy(t - 1).wait_recv()
                    solve(t - 1, True)

                @pl.when(jnp.logical_and(t == 1, turn != y))
                def _():
                    for copy in y_results():
                        copy.start()

                @pl.when(t > 1)
                def _():
                    for half in range(2):
                        dev = (x, pix(y, lax.rem(z + t, 4), half))
                        for copy in out_copies(t - 1, half, c, dev):
                            copy.start()

            @pl.when(jnp.logical_and(n == last * PARTS, turn == y))
            def _():
                for slot in range(3):
                    for copy in y_arrival(slot):
                        copy.wait_recv()
                for i in range(4):
                    for half in range(2):
                        for copy in turned(i, half):
                            copy.start()

        return carried

    lax.fori_loop(0, STEPS + LAG, step, 0)
    solve(last, False)

    twin = (x, pix(y, z, 1 - c))
    arsrc[0] = jnp.sum(arsum[...], axis=1)

    def gather(stage, peers, first):
        copies = [
            remote(arsrc.at[stage], arbuf.at[first + n], as_.at[first + n], ar_.at[first + n], dev)
            for n, dev in enumerate(peers)
        ]
        for copy in copies:
            copy.start()
        return copies

    copies = gather(0, z_peers, 0)
    twin_copies = out_copies(last, 1 - c, 0, twin)
    for copy in twin_copies:
        copy.start()
    own = pltpu.make_async_copy(res.at[last, c], coef_out.at[:, :, :, lanes(z, c)], c_loc)
    own.start()
    sstage[z * 2 + c] = sres[last, c]
    started = list(copies)
    for copy in copies:
        copy.wait_recv()
    total = arsrc[0]
    for n in range(7):
        total = total + arbuf[n]
    arsrc[1] = total
    copies = gather(1, plane_peers, 7)
    started += copies
    for copy in copies:
        copy.wait_recv()
    total = arsrc[1]
    for n in range(15):
        total = total + arbuf[7 + n]
    total = jnp.sum(total, axis=1, keepdims=True)
    inverse = 1.0 / jnp.sqrt(total / total[7:8, :])

    for t in range(last):
        for half in range(2):
            dev = (x, pix(y, lax.rem(z + 1 + t, 4), half))
            for copy in out_copies(t, half, half, dev):
                copy.wait_recv()
                if t > 0:
                    copy.wait_send()
    for copy in twin_copies:
        copy.wait()
    own.wait()
    for b in range(BANDS):
        factor_b = jnp.broadcast_to(inverse[b:b + 1, :], (8, 128))
        for n in range(8):
            score_out[b, :, n * 128:(n + 1) * 128] = sstage[n, b] * factor_b

    for copy in started:
        copy.wait_send()
    for tp in range(1, 4):
        d_remote(tp).wait_send()
        xw_copy(tp).wait_send()

    @pl.when(turn != y)
    def _():
        for copy in y_results():
            copy.wait_send()

    @pl.when(turn == y)
    def _():
        for i in range(4):
            for half in range(2):
                for copy in turned(i, half):
                    copy.wait_send()

    def drain(s, carried):
        t = lax.div(s, PARTS)
        q = lax.rem(s, PARTS)

        @pl.when(t > 0)
        def _():
            for tp in range(1, 4):
                y_copy(s, t, q, tp).wait_send()

        @pl.when(t < last)
        def _():
            a_copy(s, t, q).wait_send()
            b_copy(s, t, q).wait_send()

        @pl.when(t == last)
        def _():
            for tp in range(1, 4):
                x_copy(q, tp).wait_send()

        @pl.when(q == 0)
        def _():
            @pl.when(t > 0)
            def _():
                for tp in range(1, 4):
                    yw_copy(t, tp).wait_send()

            @pl.when(t < last)
            def _():
                for copy in (wa_copy(t), wb_copy(t), wc_copy(t), wd_copy(t), sum_copy(t)):
                    copy.wait_send()

        return carried

    lax.fori_loop(0, STEPS, drain, 0)


def local(stack, quality, days):
    design = jnp.pad(design_matrix(days), ((0, 0), (0, 120)))
    dma = pltpu.SemaphoreType.DMA
    vmem = pltpu.VMEM
    hbm = pl.BlockSpec(memory_space=pltpu.HBM)
    samples = (GROUP, BANDS, 16, 128)
    codes = (GROUP, 16, 128)
    return pl.pallas_call(
        fit_kernel,
        out_shape=(
            jax.ShapeDtypeStruct((BANDS, 8, 8, 1024), F32),
            jax.ShapeDtypeStruct((BANDS, 8, 1024), F32),
        ),
        in_specs=[hbm, hbm, hbm],
        out_specs=(hbm, pl.BlockSpec(memory_space=pltpu.VMEM)),
        scratch_shapes=[
            vmem((4, CHUNKS) + samples, BF16),
            vmem((4, CHUNKS) + codes, BF16),
            vmem((3, CHUNKS) + samples, BF16),
            vmem((3, CHUNKS) + codes, BF16),
            vmem((CHUNKS - 1,) + samples, BF16),
            vmem((CHUNKS - 1,) + codes, BF16),
            vmem((3, CHUNKS) + codes, BF16),
            vmem((GROUP, 256, 128), jnp.int32),
            vmem((4, GROUP, 128), F32),
            vmem((4, GROUP, 8, 8, 128), F32),
            vmem((CHUNKS, BANDS, 9, 16, 128), F32),
            vmem((CHUNKS - 1, BANDS, 9, 16, 128), F32),
            vmem((CHUNKS - 1, BANDS, 9, 16, 128), F32),
            vmem((CHUNKS, 36, 16, 128), F32),
            vmem((CHUNKS, 36, 16, 128), F32),
            vmem((CHUNKS, 2, BANDS, 8, 8, 128), F32),
            vmem((CHUNKS, 2, BANDS, 8, 128), F32),
            vmem((3, 2, BANDS, 8, 8, 128), F32),
            vmem((3, 2, BANDS, 8, 128), F32),
            vmem((8, BANDS, 8, 128), F32),
            vmem((8, 8, 128), F32),
            vmem((2, 8, 128), F32),
            vmem((22, 8, 128), F32),
            dma, dma((STEPS, 4)), dma,
            dma((STEPS, 3)), dma((STEPS, 3)), dma((CHUNKS, 3)), dma((CHUNKS, 3)),
            dma((STEPS,)), dma((STEPS,)), dma((STEPS,)), dma((STEPS,)), dma((PARTS, 3)), dma((PARTS, 3)),
            dma((CHUNKS,)), dma((CHUNKS,)), dma((CHUNKS, 3)), dma((CHUNKS, 3)), dma((CHUNKS,)), dma((CHUNKS,)),
            dma((3,)), dma((3,)), dma((2,)), dma((3, 2)), dma((4, 2)), dma((4, 2)),
            dma((CHUNKS, 2)), dma((CHUNKS, 2)), dma((CHUNKS, 2)), dma((CHUNKS, 2)),
            dma, dma((22,)), dma((22,)),
        ],
        compiler_params=pltpu.CompilerParams(
            collective_id=0, has_side_effects=True, vmem_limit_bytes=48 * 1024 * 1024
        ),
        name="fit",
    )(stack, quality, design)


def solution(mesh):
    return jax.shard_map(
        local,
        mesh=mesh,
        in_specs=(P("date", None, None, "pix"), P("date", None, "pix"), P("date")),
        out_specs=(P(None, None, "pix", "date"), P(None, "pix", "date")),
        check_vma=False,
    )
```

time: 130 us -> 121 us (0.931)
  Pallas kernels: 124 us -> 114 us
    pallas_call x1, Pallas kernels: 124 us -> 114 us  [local(): pl.pallas_call(fit_kernel, out_shape=(jax.ShapeDtypeStruct((BANDS, 8, 8,...]
where the time goes in v2:
time: 121 us; the launch traced here: 119 us
  Pallas kernels  114 us (94%)
  local copies, waits for them, and re-layouts  4.18 us (3%)
    pallas_call x1, Pallas kernels, local(): pl.pallas_call(fit_kernel, out_shape=(jax.ShapeDtypeStruct((BANDS, 8, 8,...  114 us
    unnamed x4, local copies, waits for them, and re-layouts  3.5 us

profile of v2, /device:TPU:1, one launch (start us, length us, event | category | flops | bytes accessed | tf_op | source)
XLA Modules:
  0.0 119.1 jit_solution(11461647012482008201)
XLA Ops:
  0.6 0.7 sine_bitcast_fusion
  1.3 0.1 copy.11
  1.4 0.1 copy.9
  1.5 0.1 copy.7
  1.6 0.1 copy.6
  1.7 0.1 copy.8
  1.8 0.1 copy.10
  1.8 0.1 copy.5
  1.9 0.1 stack.32
  2.0 0.0 copy-start
  2.0 1.6 %copy-done = s32[16,256,128]{2,1,0:T(8,128)S(1)} copy-done((s32[16,256,128]{2,1,0:T(8,128)S(1)}, s32[16,256,128]{2,1,0:T(8,128)}, u32[]{:S(2)}) %copy-start) | copy-done | bytes 2097176
  3.6 113.6 %fit.1 = (f32[7,8,8,1024]{3,2,1,0:T(8,128)S(1)}, f32[7,8,1024]{2,1,0:T(8,128)S(1)}) custom-call(bf16[16,7,256,128]{3,2,1,0:T(8,128)(2,1)} %stack.33, s32[16,256,128]{2,1,0:T(8,128)S(1)} %copy-done, f32[16,128]{1,0:T(8,128)S(1)} %pad.4.design), custom_call_target="tpu_custom_call" | custom-call | tf_op jit(solution)/shard_map/fit/pallas_call | solution.py:625
  117.2 1.2 %copy.14 = f32[7,8,8,1024]{3,2,1,0:T(8,128)} copy(f32[7,8,8,1024]{3,2,1,0:T(8,128)S(1)} %get-tuple-element.11) | data formatting | bytes 3670016
  118.4 0.7 copy.15
  (2 shorter events, 0.0 us)
Async XLA Ops:
  2.0 1.6 %copy-start = (s32[16,256,128]{2,1,0:T(8,128)S(1)}, s32[16,256,128]{2,1,0:T(8,128)}, u32[]{:S(2)}) copy-start(s32[16,256,128]{2,1,0:T(8,128)} %quality.1) | copy-start | bytes 6291460

commit v3 on v2

--- a/solution.py
+++ b/solution.py
@@ -15,8 +15,14 @@
 DPART = GROUP // PARTS
 CHUNKS = 4
 STEPS = CHUNKS * PARTS
-AHEAD = 3
+AHEAD = 7
+RAMP = 11
+EARLY = 2
 LAG = 3
+FACTOR_AT = 2
+SOLVE_AT = 1
+TURN_AT = 14
+CHAINED = 3
 SCALE = 12.0
 PAIRS = [(i, j) for i in range(8) for j in range(i, 8)]
 
@@ -83,8 +89,11 @@
     def dates(q):
         return pl.ds(q * DPART, DPART)
 
+    def row_z(t):
+        return lax.rem(z + (1 + t) * (3 - 2 * c), 4)
+
     def chunk_row(ry, t):
-        return pl.multiple_of(ry * 64 + lax.rem(z + 1 + t, 4) * 16, 16)
+        return pl.multiple_of(ry * 64 + row_z(t) * 16, 16)
 
     def first_local(q, i):
         ry = lax.rem(y + i + 2 * c, 4)
@@ -121,18 +130,18 @@
     def b_copy(s, t, q):
         return remote(mid.at[back_slot, t, dates(q)], far.at[2 * c, t, dates(q)], b_s.at[s], b_r.at[s], back_dev)
 
-    def x_copy(q, tp):
+    def x_copy(s, t, q, tp):
         i = lax.rem(x + tp - y + 4, 4)
         return remote(
-            mid.at[i, last, dates(q)], far.at[3 - tp, last, dates(q)],
-            xs.at[q, tp - 1], xr.at[q, 3 - tp], x_peers[tp - 1],
-        )
-
-    def xw_copy(tp):
+            mid.at[i, t, dates(q)], far.at[3 - tp, t, dates(q)],
+            xs.at[s, tp - 1], xr.at[s, 3 - tp], x_peers[tp - 1],
+        )
+
+    def xw_copy(t, tp):
         i = lax.rem(x + tp - y + 4, 4)
         return remote(
-            midw.at[i, last], farw.at[3 - tp, last],
-            ws.at[last, tp - 1], wr.at[last, 3 - tp], x_peers[tp - 1],
+            midw.at[i, t], farw.at[3 - tp, t],
+            ws.at[t, tp - 1], wr.at[t, 3 - tp], x_peers[tp - 1],
         )
 
     def wa_copy(t):
@@ -179,13 +188,23 @@
         pl.semaphore_signal(barrier, inc=1, device_id=dev, device_id_type=MESH)
     pl.semaphore_wait(barrier, 13)
 
+    def first_start(q):
+        for i in range(4):
+            first_local(q, i).wait()
+        a_copy(q, 0, q).start()
+        b_copy(q, 0, q).start()
+
     y_start(PARTS)
-    for i in range(4):
-        first_local(0, i).wait()
-    a_copy(0, 0, 0).start()
-    b_copy(0, 0, 0).start()
+    first_start(0)
+    for q in range(1, 1 + PARTS // 4):
+        first_start(q)
     for tp in range(1, 4):
         d_remote(tp).start()
+
+    def x_codes(t):
+        wa_copy(t).start()
+        wb_copy(t).start()
+        wc_copy(t).start()
 
     q_copy.wait()
 
@@ -212,8 +231,13 @@
 
     lax.fori_loop(0, 4 * CHUNKS, encode, 0)
     yw_start(1)
-    for s in range(1, AHEAD):
-        y_start(PARTS + s)
+    x_codes(0)
+    for q in range(1 + PARTS // 4, PARTS):
+        first_start(q)
+    for s in range(PARTS + 1, PARTS + AHEAD):
+        if s % PARTS == 0:
+            yw_start(s // PARTS)
+        y_start(s)
     arsum[...] = jnp.zeros_like(arsum)
 
     def column(g, d, i):
@@ -349,7 +373,7 @@
         )
 
     def turned(i, half):
-        dev = (lax.rem(y + i, 4), pix(y, lax.rem(z + 1, 4), half))
+        dev = (lax.rem(y + i, 4), pix(y, row_z(0), half))
         src_score = sres.at[0, half] if i == 0 else ysres.at[i - 1, half]
         src = res.at[0, half] if i == 0 else yres.at[i - 1, half]
         return (
@@ -357,52 +381,148 @@
             remote(src, coef_out.at[:, :, :, lanes(z, c)], fc.at[i, half], cr.at[0, c], dev),
         )
 
+    def due(s):
+        ramp = s - LAG + jnp.maximum(s - RAMP, 0)
+        return jnp.maximum(jnp.minimum(s - EARLY, PARTS - 1), jnp.minimum(ramp, s - 1))
+
+    def use(n, carried):
+        t = lax.div(n, PARTS)
+        q = lax.rem(n, PARTS)
+
+        @pl.when(n == 0)
+        def _():
+            columns()
+
+        @pl.when(q == 0)
+        def _():
+            own_sums[t] = jnp.zeros((BANDS, 9, 16, 128), F32)
+
+            @pl.when(t < CHAINED)
+            def _():
+                pass_sums[t] = jnp.zeros((BANDS, 9, 16, 128), F32)
+                wa_copy(t).wait_recv()
+                wd_copy(t).start()
+                wb_copy(t).wait_recv()
+
+            @pl.when(t >= CHAINED)
+            def _():
+                for tp in range(1, 4):
+                    xw_copy(t, tp).wait_recv()
+
+        @pl.when(t < CHAINED)
+        def _():
+            a_copy(n, t, q).wait_recv()
+            moments(
+                pass_sums.at[t],
+                [(mid.at[fore_slot, t], midw.at[fore_slot, t], 0), (carry.at[t], carryw.at[t], back)],
+                q,
+            )
+
+            @pl.when(q == PARTS - 1)
+            def _():
+                sum_copy(t).start()
+
+            b_copy(n, t, q).wait_recv()
+
+        @pl.when(t >= CHAINED)
+        def _():
+            for tp in range(1, 4):
+                x_copy(n, t, q, tp).wait_recv()
+            moments(
+                own_sums.at[t],
+                [(far.at[1, t], farw.at[1, t], 2), (far.at[2 - 2 * c, t], farw.at[2 - 2 * c, t], back)],
+                q,
+            )
+
+        moments(
+            own_sums.at[t],
+            [(mid.at[home, t], midw.at[home, t], 0), (far.at[2 * c, t], farw.at[2 * c, t], fore)],
+            q,
+        )
+
+        @pl.when(q == FACTOR_AT)
+        def _():
+            @pl.when(t < CHAINED)
+            def _():
+                wc_copy(t).wait_recv()
+                wd_copy(t).wait_recv()
+
+            factor(t)
+
+        def send_results(done):
+            for half in range(2):
+                dev = (x, pix(y, row_z(done), half))
+                for copy in out_copies(done, half, c, dev):
+                    copy.start()
+
+        @pl.when(jnp.logical_and(q == SOLVE_AT, jnp.logical_and(t > 0, t <= CHAINED)))
+        def _():
+            sum_copy(t - 1).wait_recv()
+            solve(t - 1, True)
+
+            @pl.when(jnp.logical_and(t == 1, turn != y))
+            def _():
+                for copy in y_results():
+                    copy.start()
+
+            @pl.when(t > 1)
+            def _():
+                send_results(t - 1)
+
+        @pl.when(jnp.logical_and(q == PARTS - 1, t >= CHAINED))
+        def _():
+            solve(t, False)
+
+            @pl.when(t < last)
+            def _():
+                send_results(t)
+
+        @pl.when(jnp.logical_and(n == TURN_AT, turn == y))
+        def _():
+            for slot in range(3):
+                for copy in y_arrival(slot):
+                    copy.wait_recv()
+            for i in range(4):
+                for half in range(2):
+                    for copy in turned(i, half):
+                        copy.start()
+
+        return carried
+
     def step(s, carried):
-        @pl.when(s < STEPS)
+        @pl.when(jnp.logical_and(s >= PARTS, s < STEPS))
         def _():
             t = lax.div(s, PARTS)
             q = lax.rem(s, PARTS)
-
-            @pl.when(jnp.logical_and(t == 0, q > 0))
-            def _():
-                for i in range(4):
-                    first_local(q, i).wait()
-
-            @pl.when(t > 0)
-            def _():
-                y_local(s, t, q).wait()
-                for tp in range(1, 4):
-                    y_copy(s, t, q, tp).wait_recv()
-
-            @pl.when(jnp.logical_and(s > 0, t < last))
+            y_local(s, t, q).wait()
+            for tp in range(1, 4):
+                y_copy(s, t, q, tp).wait_recv()
+
+            @pl.when(t < CHAINED)
             def _():
                 a_copy(s, t, q).start()
                 b_copy(s, t, q).start()
 
-            @pl.when(t == last)
+            @pl.when(t >= CHAINED)
             def _():
                 for tp in (2, 1, 3):
-                    x_copy(q, tp).start()
+                    x_copy(s, t, q, tp).start()
 
             @pl.when(q == 0)
             def _():
-                @pl.when(t > 0)
+                for tp in range(1, 4):
+                    yw_copy(t, tp).wait_recv()
+
+                @pl.when(t < CHAINED)
                 def _():
-                    for tp in range(1, 4):
-                        yw_copy(t, tp).wait_recv()
-
-                @pl.when(t < last)
-                def _():
-                    wa_copy(t).start()
-                    wb_copy(t).start()
-                    wc_copy(t).start()
-
-                @pl.when(t == last)
+                    x_codes(t)
+
+                @pl.when(t >= CHAINED)
                 def _():
                     for tp in (2, 1, 3):
-                        xw_copy(tp).start()
-
-            nxt = s + PARTS + AHEAD
+                        xw_copy(t, tp).start()
+
+            nxt = s + AHEAD
 
             @pl.when(nxt < STEPS)
             def _():
@@ -412,103 +532,10 @@
 
                 y_start(nxt)
 
-        @pl.when(s >= LAG)
-        def _():
-            n = s - LAG
-            t = lax.div(n, PARTS)
-            q = lax.rem(n, PARTS)
-
-            @pl.when(n == 0)
-            def _():
-                columns()
-
-            @pl.when(q == 0)
-            def _():
-                own_sums[t] = jnp.zeros((BANDS, 9, 16, 128), F32)
-
-                @pl.when(t < last)
-                def _():
-                    pass_sums[t] = jnp.zeros((BANDS, 9, 16, 128), F32)
-                    wa_copy(t).wait_recv()
-                    wd_copy(t).start()
-                    wb_copy(t).wait_recv()
-
-                @pl.when(t == last)
-                def _():
-                    for tp in range(1, 4):
-                        xw_copy(tp).wait_recv()
-
-            @pl.when(t < last)
-            def _():
-                a_copy(n, t, q).wait_recv()
-                moments(
-                    pass_sums.at[t],
-                    [(mid.at[fore_slot, t], midw.at[fore_slot, t], 0), (carry.at[t], carryw.at[t], back)],
-                    q,
-                )
-
-                @pl.when(q == PARTS - 1)
-                def _():
-                    sum_copy(t).start()
-
-                b_copy(n, t, q).wait_recv()
-
-            @pl.when(t == last)
-            def _():
-                for tp in range(1, 4):
-                    x_copy(q, tp).wait_recv()
-                moments(
-                    own_sums.at[t],
-                    [(far.at[1, t], farw.at[1, t], 2), (far.at[2 - 2 * c, t], farw.at[2 - 2 * c, t], back)],
-                    q,
-                )
-
-            moments(
-                own_sums.at[t],
-                [(mid.at[home, t], midw.at[home, t], 0), (far.at[2 * c, t], farw.at[2 * c, t], fore)],
-                q,
-            )
-
-            @pl.when(q == PARTS - 2)
-            def _():
-                @pl.when(t < last)
-                def _():
-                    wc_copy(t).wait_recv()
-                    wd_copy(t).wait_recv()
-
-                factor(t)
-
-                @pl.when(t > 0)
-                def _():
-                    sum_copy(t - 1).wait_recv()
-                    solve(t - 1, True)
-
-                @pl.when(jnp.logical_and(t == 1, turn != y))
-                def _():
-                    for copy in y_results():
-                        copy.start()
-
-                @pl.when(t > 1)
-                def _():
-                    for half in range(2):
-                        dev = (x, pix(y, lax.rem(z + t, 4), half))
-                        for copy in out_copies(t - 1, half, c, dev):
-                            copy.start()
-
-            @pl.when(jnp.logical_and(n == last * PARTS, turn == y))
-            def _():
-                for slot in range(3):
-                    for copy in y_arrival(slot):
-                        copy.wait_recv()
-                for i in range(4):
-                    for half in range(2):
-                        for copy in turned(i, half):
-                            copy.start()
-
+        lax.fori_loop(due(s - 1) + 1, due(s) + 1, use, 0)
         return carried
 
-    lax.fori_loop(0, STEPS + LAG, step, 0)
-    solve(last, False)
+    lax.fori_loop(EARLY, STEPS + 1, step, 0)
 
     twin = (x, pix(y, z, 1 - c))
     arsrc[0] = jnp.sum(arsum[...], axis=1)
@@ -548,7 +575,7 @@
 
     for t in range(last):
         for half in range(2):
-            dev = (x, pix(y, lax.rem(z + 1 + t, 4), half))
+            dev = (x, pix(y, row_z(t), half))
             for copy in out_copies(t, half, half, dev):
                 copy.wait_recv()
                 if t > 0:
@@ -565,7 +592,6 @@
         copy.wait_send()
     for tp in range(1, 4):
         d_remote(tp).wait_send()
-        xw_copy(tp).wait_send()
 
     @pl.when(turn != y)
     def _():
@@ -588,15 +614,15 @@
             for tp in range(1, 4):
                 y_copy(s, t, q, tp).wait_send()
 
-        @pl.when(t < last)
+        @pl.when(t < CHAINED)
         def _():
             a_copy(s, t, q).wait_send()
             b_copy(s, t, q).wait_send()
 
-        @pl.when(t == last)
+        @pl.when(t >= CHAINED)
         def _():
             for tp in range(1, 4):
-                x_copy(q, tp).wait_send()
+                x_copy(s, t, q, tp).wait_send()
 
         @pl.when(q == 0)
         def _():
@@ -605,10 +631,15 @@
                 for tp in range(1, 4):
                     yw_copy(t, tp).wait_send()
 
-            @pl.when(t < last)
+            @pl.when(t < CHAINED)
             def _():
                 for copy in (wa_copy(t), wb_copy(t), wc_copy(t), wd_copy(t), sum_copy(t)):
                     copy.wait_send()
+
+            @pl.when(t >= CHAINED)
+            def _():
+                for tp in range(1, 4):
+                    xw_copy(t, tp).wait_send()
 
         return carried
 
@@ -635,15 +666,15 @@
             vmem((4, CHUNKS) + codes, BF16),
             vmem((3, CHUNKS) + samples, BF16),
             vmem((3, CHUNKS) + codes, BF16),
-            vmem((CHUNKS - 1,) + samples, BF16),
-            vmem((CHUNKS - 1,) + codes, BF16),
+            vmem((CHAINED,) + samples, BF16),
+            vmem((CHAINED,) + codes, BF16),
             vmem((3, CHUNKS) + codes, BF16),
             vmem((GROUP, 256, 128), jnp.int32),
             vmem((4, GROUP, 128), F32),
             vmem((4, GROUP, 8, 8, 128), F32),
             vmem((CHUNKS, BANDS, 9, 16, 128), F32),
-            vmem((CHUNKS - 1, BANDS, 9, 16, 128), F32),
-            vmem((CHUNKS - 1, BANDS, 9, 16, 128), F32),
+            vmem((CHAINED, BANDS, 9, 16, 128), F32),
+            vmem((CHAINED, BANDS, 9, 16, 128), F32),
             vmem((CHUNKS, 36, 16, 128), F32),
             vmem((CHUNKS, 36, 16, 128), F32),
             vmem((CHUNKS, 2, BANDS, 8, 8, 128), F32),
@@ -656,7 +687,7 @@
             vmem((22, 8, 128), F32),
             dma, dma((STEPS, 4)), dma,
             dma((STEPS, 3)), dma((STEPS, 3)), dma((CHUNKS, 3)), dma((CHUNKS, 3)),
-            dma((STEPS,)), dma((STEPS,)), dma((STEPS,)), dma((STEPS,)), dma((PARTS, 3)), dma((PARTS, 3)),
+            dma((STEPS,)), dma((STEPS,)), dma((STEPS,)), dma((STEPS,)), dma((STEPS, 3)), dma((STEPS, 3)),
             dma((CHUNKS,)), dma((CHUNKS,)), dma((CHUNKS, 3)), dma((CHUNKS, 3)), dma((CHUNKS,)), dma((CHUNKS,)),
             dma((3,)), dma((3,)), dma((2,)), dma((3, 2)), dma((4, 2)), dma((4, 2)),
             dma((CHUNKS, 2)), dma((CHUNKS, 2)), dma((CHUNKS, 2)), dma((CHUNKS, 2)),

time: 121 us -> 117 us (0.967); the launches traced: 119 us -> 117 us
  Pallas kernels: 114 us -> 111 us
    pallas_call x1, Pallas kernels: 114 us -> 111 us  [local(): pl.pallas_call(fit_kernel, out_shape=(jax.ShapeDtypeStruct((BANDS, 8, 8,...]
where the time goes in v3:
time: 117 us
  Pallas kernels  111 us (95%)
  local copies, waits for them, and re-layouts  4.18 us (4%)
    pallas_call x1, Pallas kernels, local(): pl.pallas_call(fit_kernel, out_shape=(jax.ShapeDtypeStruct((BANDS, 8, 8,...  111 us
    unnamed x4, local copies, waits for them, and re-layouts  3.5 us

profile of v3, /device:TPU:1, one launch (start us, length us, event | category | flops | bytes accessed | tf_op | source)
XLA Modules:
  0.0 116.7 jit_solution(2192948290087510867)
XLA Ops:
  0.6 0.7 sine_bitcast_fusion
  1.3 0.1 copy.11
  1.4 0.1 copy.9
  1.5 0.1 copy.7
  1.6 0.1 copy.6
  1.7 0.1 copy.8
  1.8 0.1 copy.10
  1.8 0.1 copy.5
  1.9 0.1 stack.32
  2.0 0.0 copy-start
  2.0 1.6 %copy-done = s32[16,256,128]{2,1,0:T(8,128)S(1)} copy-done((s32[16,256,128]{2,1,0:T(8,128)S(1)}, s32[16,256,128]{2,1,0:T(8,128)}, u32[]{:S(2)}) %copy-start) | copy-done | bytes 2097176
  3.6 111.1 %fit.1 = (f32[7,8,8,1024]{3,2,1,0:T(8,128)S(1)}, f32[7,8,1024]{2,1,0:T(8,128)S(1)}) custom-call(bf16[16,7,256,128]{3,2,1,0:T(8,128)(2,1)} %stack.33, s32[16,256,128]{2,1,0:T(8,128)S(1)} %copy-done, f32[16,128]{1,0:T(8,128)S(1)} %pad.4.design), custom_call_target="tpu_custom_call" | custom-call | tf_op jit(solution)/shard_map/fit/pallas_call | solution.py:656
  114.8 1.2 %copy.14 = f32[7,8,8,1024]{3,2,1,0:T(8,128)} copy(f32[7,8,8,1024]{3,2,1,0:T(8,128)S(1)} %get-tuple-element.11) | data formatting | bytes 3670016
  116.0 0.7 copy.15
  (2 shorter events, 0.0 us)
Async XLA Ops:
  2.0 1.6 %copy-start = (s32[16,256,128]{2,1,0:T(8,128)S(1)}, s32[16,256,128]{2,1,0:T(8,128)}, u32[]{:S(2)}) copy-start(s32[16,256,128]{2,1,0:T(8,128)} %quality.1) | copy-start | bytes 6291460

commit v4 on v3

--- a/solution.py
+++ b/solution.py
@@ -33,12 +33,11 @@
 
 def design_matrix(days):
     moment_t = days.astype(F32)
-    columns = [jnp.ones_like(moment_t), (moment_t - 512.0) / 512.0]
-    for order in range(1, 4):
-        phase = 2.0 * jnp.pi * order * moment_t / 365.25
-        columns.append(jnp.cos(phase))
-        columns.append(jnp.sin(phase))
-    return jnp.stack(columns, 1)
+    lane = lax.broadcasted_iota(jnp.int32, (GROUP, 128), 1)
+    rate = jnp.where(lane < 4, 2.0 * jnp.pi, jnp.where(lane < 6, 4.0 * jnp.pi, 6.0 * jnp.pi)).astype(F32)
+    phase = rate * moment_t / 365.25
+    wave = jnp.where(jnp.bitwise_and(lane, 1) == 0, jnp.cos(phase), jnp.sin(phase))
+    return jnp.where(lane == 0, 1.0, jnp.where(lane == 1, (moment_t - 512.0) / 512.0, wave))
 
 
 def fit_kernel(
@@ -647,7 +646,7 @@
 
 
 def local(stack, quality, days):
-    design = jnp.pad(design_matrix(days), ((0, 0), (0, 120)))
+    design = design_matrix(lax.optimization_barrier(jnp.broadcast_to(days[:, None], (GROUP, 128))))
     dma = pltpu.SemaphoreType.DMA
     vmem = pltpu.VMEM
     hbm = pl.BlockSpec(memory_space=pltpu.HBM)
@@ -694,7 +693,7 @@
             dma, dma((22,)), dma((22,)),
         ],
         compiler_params=pltpu.CompilerParams(
-            collective_id=0, has_side_effects=True, vmem_limit_bytes=48 * 1024 * 1024
+            collective_id=0, has_side_effects=True, vmem_limit_bytes=50 * 1024 * 1024
         ),
         name="fit",
     )(stack, quality, design)

time: 117 us -> 115 us (0.983)
  local copies, waits for them, and re-layouts: 4.18 us -> 2.65 us
    unnamed x4 -> x2, local copies, waits for them, and re-layouts: 3.5 us -> 1.92 us
where the time goes in v4:
time: 115 us
  Pallas kernels  111 us (97%)
  local copies, waits for them, and re-layouts  2.65 us (2%)
    pallas_call x1, Pallas kernels, local(): pl.pallas_call(fit_kernel, out_shape=(jax.ShapeDtypeStruct((BANDS, 8, 8,...  111 us

profile of v4, /device:TPU:1, one launch (start us, length us, event | category | flops | bytes accessed | tf_op | source)
XLA Modules:
  0.0 114.5 jit_solution(15632837730664892000)
XLA Ops:
  0.7 0.7 broadcast_in_dim.23
  1.4 0.1 select_select_fusion.design
  1.5 111.1 %fit.1 = (f32[7,8,8,1024]{3,2,1,0:T(8,128)S(1)}, f32[7,8,1024]{2,1,0:T(8,128)S(1)}) custom-call(bf16[16,7,256,128]{3,2,1,0:T(8,128)(2,1)} %stack.1, s32[16,256,128]{2,1,0:T(8,128)} %quality.1, f32[16,128]{1,0:T(8,128)S(1)} %select_select_fusion.design), custom_call_target="tpu_custom_call" | custom-call | tf_op jit(solution)/shard_map/fit/pallas_call | solution.py:655
  112.6 1.2 %copy.7 = f32[7,8,8,1024]{3,2,1,0:T(8,128)} copy(f32[7,8,8,1024]{3,2,1,0:T(8,128)S(1)} %get-tuple-element.8) | data formatting | bytes 3670016
  113.8 0.7 copy.8
  (3 shorter events, 0.0 us)

commit v5 on v4

--- a/solution.py
+++ b/solution.py
@@ -439,7 +439,7 @@
             q,
         )
 
-        @pl.when(q == FACTOR_AT)
+        @pl.when(q == jnp.where(t == last, 1, FACTOR_AT))
         def _():
             @pl.when(t < CHAINED)
             def _():

time: 115 us -> 115 us (level)
  no operation moved by 1% of the time
where the time goes in v5:
time: 115 us
  Pallas kernels  111 us (97%)
  local copies, waits for them, and re-layouts  2.65 us (2%)
    pallas_call x1, Pallas kernels, local(): pl.pallas_call(fit_kernel, out_shape=(jax.ShapeDtypeStruct((BANDS, 8, 8,...  111 us

profile of v5, /device:TPU:1, one launch (start us, length us, event | category | flops | bytes accessed | tf_op | source)
XLA Modules:
  0.0 114.5 jit_solution(18065957891947150634)
XLA Ops:
  0.7 0.7 broadcast_in_dim.23
  1.4 0.1 select_select_fusion.design
  1.5 111.1 %fit.1 = (f32[7,8,8,1024]{3,2,1,0:T(8,128)S(1)}, f32[7,8,1024]{2,1,0:T(8,128)S(1)}) custom-call(bf16[16,7,256,128]{3,2,1,0:T(8,128)(2,1)} %stack.1, s32[16,256,128]{2,1,0:T(8,128)} %quality.1, f32[16,128]{1,0:T(8,128)S(1)} %select_select_fusion.design), custom_call_target="tpu_custom_call" | custom-call | tf_op jit(solution)/shard_map/fit/pallas_call | solution.py:655
  112.6 1.2 %copy.7 = f32[7,8,8,1024]{3,2,1,0:T(8,128)} copy(f32[7,8,8,1024]{3,2,1,0:T(8,128)S(1)} %get-tuple-element.8) | data formatting | bytes 3670016
  113.8 0.7 copy.8
  (3 shorter events, 0.0 us)
